TPU v7x, 128 devices: a whole 4x4x4 slice. The times are simulated.
128 devices in a mesh: row: 8 (over y, core), col: 16 (over z, x).
Axes of the slice: x: 4, y: 4, z: 4, core: 2. Of those that a mesh axis runs over, the one named last changes fastest.
Arguments:
- parent_front: float32 [8, 2048, 4, 4096], P(None, 'row', None, 'col'), may hold values from -6 to 6
- generators: bfloat16 [96, 256, 256], P('row'), may hold values from -1.5 to 1.5
- diagonal_blocks: bfloat16 [96, 256, 256], P('row'), may hold values from -6 to 6
- coupling: bfloat16 [2, 256, 256], replicated, may hold values from -0.375 to 0.375
- block_map: int32 [2, 48], replicated, may hold values from 0 to 63, as said below
- valid_rows: int32 [2, 48], replicated, may hold values from 128 to 256
Outputs:
- assembled: float32 [8, 2048, 4, 4096], P(None, 'row', None, 'col')
Inputs may be any that keep to these rules, and one draw needn't show every extreme that they name: `block_map`: for each child c and each s < 4, the child blocks s * 12 to (s + 1) * 12 - 1 map in increasing order to distinct parent blocks of the range s * 16 to (s + 1) * 16 - 1, and the parent blocks s * 16 + m * 8 of that range always receive one.
All inputs are finite; a program needn't handle non-finite values.
Results may differ from a plain program's by a relative error of at most 0.0028.
Values may be sent and summed in bfloat16 or wider, within the bound.
No kernel may reach another device: no remote copies, remote signals or barrier semaphores. Data moves between devices by JAX's collectives and lax.ppermute only.
A program may use at most 128 MiB of HBM per device.

v0:
```python
import jax
import jax.numpy as jnp
from jax import lax
from jax.sharding import PartitionSpec as P


def sent_together(arrays, axis, dim, along):
    both = jnp.concatenate(arrays, axis=along)
    filled, at, outs = (lax.all_gather(both, axis, axis=dim, tiled=True), 0, [])
    for a in arrays:
        outs.append(lax.slice_in_dim(filled, at, at + a.shape[along], axis=along))
        at += a.shape[along]
    return tuple(outs)


def split_children(stacked, half_rows):
    grouped = stacked.reshape((half_rows, 2, -1) + stacked.shape[2:])
    grouped = jnp.swapaxes(grouped, 0, 1)
    return grouped.reshape((2, -1) + stacked.shape[2:])


def shards(parent_front, generators, diagonal_blocks, coupling, block_map, valid_rows):
    row_count = lax.axis_size("row")
    col_count = lax.axis_size("col")
    half_rows = row_count // 2
    row_index = lax.axis_index("row")
    col_index = lax.axis_index("col")
    own_child = row_index % 2
    own_group = row_index // 2
    group_blocks = generators.shape[0]
    block_size = generators.shape[1]
    rank_width = generators.shape[2]
    rows_local = parent_front.shape[0]
    cols_local = parent_front.shape[2]
    window = 2 * rows_local
    row_cap = window // row_count
    col_cap = window // col_count
    map_child = lax.dynamic_index_in_dim(block_map, own_child, 0, keepdims=False)
    count_child = lax.dynamic_index_in_dim(valid_rows, own_child, 0, keepdims=False)
    coupling_own = lax.dynamic_index_in_dim(coupling, own_child, 0, keepdims=False)
    group_start = own_group * group_blocks
    map_group = lax.dynamic_slice_in_dim(map_child, group_start, group_blocks)
    count_group = lax.dynamic_slice_in_dim(count_child, group_start, group_blocks)
    row_offsets = jnp.arange(block_size, dtype=jnp.int32)
    kept_mask = (row_offsets[None, :] < count_group[:, None]).astype(jnp.bfloat16)
    masked = generators * kept_mask[:, :, None]
    projected = jnp.einsum(
        "ixq,qr->ixr", masked, coupling_own, preferred_element_type=jnp.float32
    ).astype(jnp.bfloat16)
    diag_kept = diagonal_blocks * kept_mask[:, :, None] * kept_mask[:, None, :]
    window_pos = map_group - own_group * window
    slot_ids = jnp.arange(window, dtype=jnp.int32)
    window_place = (window_pos[None, :] == slot_ids[:, None]).astype(jnp.bfloat16)
    row_place = window_place.reshape(row_cap, row_count, group_blocks)
    row_send = jnp.einsum(
        "kri,ixq->rkxq", row_place, masked, preferred_element_type=jnp.float32
    ).astype(jnp.bfloat16)
    row_received = lax.all_to_all(row_send, "row", split_axis=0, concat_axis=0, tiled=True)
    row_received = split_children(row_received, half_rows)
    wanted = jnp.arange(col_cap, dtype=jnp.int32) * col_count + col_index
    column_pick = (window_pos[None, :] == wanted[:, None]).astype(jnp.bfloat16)
    col_send = jnp.einsum(
        "ki,izq->kzq", column_pick, projected, preferred_element_type=jnp.float32
    ).astype(jnp.bfloat16)
    diag_send = jnp.einsum(
        "ki,ixz->kxz", column_pick, diag_kept, preferred_element_type=jnp.float32
    ).astype(jnp.bfloat16)
    col_received, diag_received = sent_together((col_send, diag_send), "row", 0, 1)
    col_received = split_children(
        col_received.reshape(row_count, col_cap, block_size, rank_width), half_rows
    )
    diag_received = split_children(
        diag_received.reshape(row_count, col_cap, block_size, block_size), half_rows
    )
    row_parents = jnp.arange(rows_local, dtype=jnp.int32) * row_count + row_index
    col_parents = jnp.arange(cols_local, dtype=jnp.int32) * col_count + col_index
    on_diag = (row_parents[:, None] == col_parents[None, :]).astype(jnp.float32)
    running = parent_front
    for child_index in range(2):
        child_tile = jnp.einsum(
            "axq,bzq->axbz",
            row_received[child_index],
            col_received[child_index],
            preferred_element_type=jnp.float32,
        )
        diag_part = diag_received[child_index].astype(jnp.float32).transpose(1, 0, 2)
        child_tile = child_tile + on_diag[:, None, :, None] * diag_part[None]
        rounded = lax.optimization_barrier(child_tile.astype(jnp.bfloat16))
        running = running + rounded.astype(jnp.float32)
    return running


def solution(mesh):
    in_specs = (
        P(None, "row", None, "col"),
        P("row", None, None),
        P("row", None, None),
        P(),
        P(),
        P(),
    )
    out_specs = P(None, "row", None, "col")
    return jax.shard_map(shards, mesh=mesh, in_specs=in_specs, out_specs=out_specs, check_vma=False)
```

profile of v0, /device:TPU:0, one launch (start us, length us, event | category | flops | bytes accessed | tf_op | source)
XLA Modules:
  0.0 94.3 jit_solution(12038976815060474854)
XLA Ops:
  6.5 0.0 copy-start
  6.5 0.0 copy-start.1
  6.5 0.0 all-gather.2.cloned.1.call-start
  6.5 0.0 copy-start.2
  6.5 0.9 dynamic-slice_bitcast_fusion
  7.5 0.1 fusion.15
  7.5 0.0 copy-done
  7.5 2.1 %convolution_convert_fusion = bf16[12,256,256]{2,1,0:T(8,128)(2,1)S(1)} fusion(bf16[12,256,256]{2,1,0:T(8,128)(2,1)} %param.7, bf16[12,256]{1,0:T(8,128)(2,1)S(1)} %fusion.15, bf16[2,256,256]{2,1,0:T(8,128)(2,1)S(1)} %copy-done, s32[]{:T(128)S(6)} %select_n.27), kind=kOutput, calls=%fused_computation.12 | convolution fusion | flops 404226048 | bytes 3284996 | tf_op jit(solution)/shard_map/ixq,qr->ixr/dot_general | solution.py:47
  9.6 0.0 copy-done.1
  9.6 0.0 copy-done.2
  9.6 0.0 copy-start.3
  9.6 0.6 multiply_bitcast_fusion
  10.3 0.1 copy-done.3
  10.3 1.0 %fusion.5 = bf16[1,256,256]{2,0,1:T(2,128)(2,1)S(1)} fusion(bf16[12,256,256]{2,1,0:T(8,128)(2,1)S(1)} %convolution_convert_fusion, s32[]{:T(128)S(6)} %axis_index.25, s32[2,48]{1,0:T(2,128)S(1)} %copy-done.3, s32[]{:T(128)S(6)} %select_n.28, s32[]{:T(128)S(6)} %select_n.31, s32[]{:T(128)S(6)} %mul.69), kind=kOutput, calls=%fused_computation.8 | convolution fusion | flops 1572888 | bytes 1704464 | tf_op jit(solution)/shard_map/ki,izq->kzq/dot_general | solution.py:62
  11.3 1.0 %fusion.3 = bf16[1,256,256]{2,0,1:T(2,128)(2,1)S(1)} fusion(bf16[12,256,256]{2,1,0:T(8,128)(2,1)S(1)} %get-tuple-element.12, s32[]{:T(128)S(6)} %axis_index.25, s32[2,48]{1,0:T(2,128)S(1)} %copy-done.3, s32[]{:T(128)S(6)} %select_n.28, s32[]{:T(128)S(6)} %select_n.31, s32[]{:T(128)S(6)} %mul.69), kind=kOutput, calls=%fused_computation.6 | convolution fusion | flops 1572888 | bytes 1704464 | tf_op jit(solution)/shard_map/ki,ixz->kxz/dot_general | solution.py:65
  12.4 0.7 pad_maximum_fusion
  13.1 0.0 all-gather.2.cloned.1.call-update
  13.2 0.1 fusion.31
  13.3 1.1 %convert_bitcast_fusion = bf16[8,2,256,256]{3,0,1,2:T(8,128)(2,1)S(1)} fusion(bf16[12,256,256,1]{2,1,0,3:T(8,128)(2,1)S(1)} %get-tuple-element.11, s32[2,8]{1,0:T(2,128)S(1)} %multiply_add_fusion, s32[12]{0:T(128)S(1)} %fusion.31), kind=kOutput, calls=%fused_computation.11 | convolution fusion | flops 26214592 | bytes 3670128 | tf_op jit(solution)/shard_map/kri,ixq->rkxq/dot_general | solution.py:55
  14.4 2.9 %copy.19 = bf16[8,2,256,256]{3,1,2,0:T(2,128)(2,1)} copy(bf16[8,2,256,256]{3,0,1,2:T(8,128)(2,1)S(1)} %convert_bitcast_fusion) | data formatting | bytes 4194304 | tf_op jit(solution)/shard_map/convert_element_type | solution.py:57
  17.4 4.6 %all-to-all-start = ((bf16[8,2,256,256]{3,1,2,0:T(2,128)(2,1)}), bf16[8,2,256,256]{3,1,2,0:T(2,128)(2,1)S(1)}, u32[]{:S(2)}, u32[]{:S(2)}) async-start(bf16[8,2,256,256]{3,1,2,0:T(2,128)(2,1)} %copy.19), calls=%async_computation | async-start | bytes 4194304 | tf_op jit(solution)/shard_map/all_to_all | solution.py:58
  22.0 0.1 compare_convert_fusion
  22.0 35.5 %all-to-all-done = bf16[8,2,256,256]{3,1,2,0:T(2,128)(2,1)S(1)} async-done(((bf16[8,2,256,256]{3,1,2,0:T(2,128)(2,1)}), bf16[8,2,256,256]{3,1,2,0:T(2,128)(2,1)S(1)}, u32[]{:S(2)}, u32[]{:S(2)}) %all-to-all-start) | async-done | bytes 2097184 | tf_op jit(solution)/shard_map/all_to_all | solution.py:58
  57.5 0.3 copy.52
  57.9 0.1 fusion.27
  58.0 0.0 all-gather.2.cloned.1.call-done
  58.0 1.7 %fusion.28 = (bf16[8,256,256]{2,1,0:T(8,128)(2,1)S(1)}, bf16[8,256,256]{2,1,0:T(8,128)(2,1)S(1)}) fusion(bf16[8,512,256]{2,1,0:T(8,128)(2,1)} %all-gather.2.cloned.1.call-done), kind=kLoop, calls=%fused_computation.51 | loop fusion | bytes 4194304 | tf_op jit(solution)/shard_map/slice | solution.py:11
  59.7 0.1 copy.53
  59.8 0.2 convert_bitcast_fusion.2
  60.0 1.4 %add_convert_fusion.1 = bf16[8,256,4,256]{3,1,2,0:T(8,128)(2,1)S(1)} fusion(f32[256,4,256]{2,0,1:T(8,128)S(1)} %get-tuple-element.9, f32[8,4]{1,0:T(8,128)S(1)} %compare_convert_fusion, bf16[8,256,256,1]{2,1,3,0:T(8,128)(2,1)S(1)} %bitcast.89, bf16[2,4,1,256,256]{4,3,1,2,0:T(8,128)(2,1)S(1)} %bitcast.86), kind=kOutput, calls=%fused_computation.3 | convolution fusion | flops 1080033280 | bytes 6819840 | tf_op jit(solution)/shard_map/axq,bzq->axbz/dot_general | solution.py:80
  61.4 3.4 %add_convert_fusion = bf16[8,256,4,256]{3,1,2,0:T(8,128)(2,1)} fusion(f32[256,4,256]{2,0,1:T(8,128)S(1)} %get-tuple-element.10, f32[8,4]{1,0:T(8,128)S(1)} %compare_convert_fusion, bf16[8,256,256,1]{2,1,3,0:T(8,128)(2,1)S(1)} %bitcast.88, bf16[2,4,1,256,256]{4,3,1,2,0:T(8,128)(2,1)S(1)} %bitcast.87), kind=kOutput, calls=%fused_computation.2 | convolution fusion | flops 1080033280 | bytes 6819840 | tf_op jit(solution)/shard_map/axq,bzq->axbz/dot_general | solution.py:80
  64.9 10.5 %fusion = f32[8,256,4,256]{3,1,2,0:T(8,128)} fusion(f32[8,256,4,256]{3,2,1,0:T(4,128)} %param.6, bf16[8,256,4,256]{3,1,2,0:T(8,128)(2,1)} %add_convert_fusion, bf16[8,256,4,256]{3,1,2,0:T(8,128)(2,1)S(1)} %add_convert_fusion.1), kind=kLoop, calls=%fused_computation.1 | loop fusion | flops 8388608 | bytes 25165824 | tf_op jit(solution)/shard_map/add | solution.py:89
  75.3 12.2 %copy.23 = f32[8,256,4,256]{3,2,1,0:T(4,128)} copy(f32[8,256,4,256]{3,1,2,0:T(8,128)} %fusion) | data formatting | bytes 16777216 | tf_op jit(solution)/shard_map/add | solution.py:89
  (4 shorter events, 0.1 us)
Async XLA Ops:
  6.5 1.0 %copy-start = (bf16[2,256,256]{2,1,0:T(8,128)(2,1)S(1)}, bf16[2,256,256]{2,1,0:T(8,128)(2,1)}, u32[]{:S(2)}) copy-start(bf16[2,256,256]{2,1,0:T(8,128)(2,1)} %param.9) | copy-start | bytes 786436
  6.5 3.1 %copy-start.1 = (bf16[12,256,256]{2,1,0:T(8,128)(2,1)S(1)}, bf16[12,256,256]{2,1,0:T(8,128)(2,1)}, u32[]{:S(2)}) copy-start(bf16[12,256,256]{2,1,0:T(8,128)(2,1)} %param.7) | copy-start | bytes 4718596
  6.5 51.5 %all-gather.2.cloned.1.call-start = ((), (), s32[]{:S(2)}) async-start(), calls=%async_computation.1 | async-start | bytes 2359296 | tf_op jit(solution)/shard_map/all_gather | solution.py:9
  6.5 3.1 %copy-start.2 = (bf16[12,256,256]{2,1,0:T(8,128)(2,1)S(1)}, bf16[12,256,256]{2,1,0:T(8,128)(2,1)}, u32[]{:S(2)}) copy-start(bf16[12,256,256]{2,1,0:T(8,128)(2,1)} %param.8) | copy-start | bytes 4718596
  9.6 0.7 copy-start.3
  17.4 40.2 %all-to-all-start = ((bf16[8,2,256,256]{3,1,2,0:T(2,128)(2,1)}), bf16[8,2,256,256]{3,1,2,0:T(2,128)(2,1)S(1)}, u32[]{:S(2)}, u32[]{:S(2)}) async-start(bf16[8,2,256,256]{3,1,2,0:T(2,128)(2,1)} %copy.19), calls=%async_computation | async-start | bytes 4194304 | tf_op jit(solution)/shard_map/all_to_all | solution.py:58
Sparse Core Ops, SparseCore 0:
  13.3 35.9 all-gather.1
where the time goes:
time: 95 us; the launch traced here: 94.3 us
  waiting for transfers between devices  35.5 us (37%)
  local copies, waits for them, and re-layouts  18.4 us (19%)
  between operations  13.5 us (14%)
  other arithmetic  12.2 us (13%)
  matrix products  10.1 us (11%)
  starting transfers between devices  4.58 us (5%)
    all_to_all x1, waiting for transfers between devices, shards(): lax.all_to_all(row_send, 'row', split_axis=0, concat_axis=0, tiled=True)  35.5 us
    add x1, local copies, waits for them, and re-layouts, shards(): running = running + rounded.astype(jnp.float32)  12.2 us
    add x1, other arithmetic, shards(): running = running + rounded.astype(jnp.float32)  10.5 us
    dot_general x2, matrix products, shards(): jnp.einsum('axq,bzq->axbz', row_received[child_index], col_received[child...  4.84 us
    all_to_all x1, starting transfers between devices, shards(): lax.all_to_all(row_send, 'row', split_axis=0, concat_axis=0, tiled=True)  4.58 us
    convert_element_type x1, local copies, waits for them, and re-layouts, shards(): row_send = jnp.einsum('kri,ixq->rkxq', row_place, masked, preferred_eleme...  2.94 us
    dot_general x1, matrix products, shards(): jnp.einsum('ixq,qr->ixr', masked, coupling_own, preferred_element_type=jn...  2.07 us
  transfers between devices with their start and end apart: 2, of which 1 were waited for; matrix products, arithmetic and copies ran while one was open for 5% of the time, Pallas kernels for 0%

commit v1 on v0

v1 whole, which is shorter than its diff:
```python
import functools

import jax
import jax.numpy as jnp
from jax import lax
from jax.experimental import pallas as pl
from jax.experimental.pallas import tpu as pltpu
from jax.sharding import PartitionSpec as P

Y, Z, X, BLK = 4, 4, 4, 256
QUART = BLK // 8
WIN, CG = 16, 12


def pairs(move):
    out = []
    for y in range(Y):
        for k in range(2):
            for z in range(Z):
                for x in range(X):
                    b = move(y, k, z, x)
                    source = (2 * y + k) * Z * X + z * X + x
                    target = (2 * (b[0] % Y) + b[1]) * Z * X + (b[2] % Z) * X + b[3] % X
                    out.append((source, target))
    return out


def shift(value, move):
    return lax.ppermute(value, ("row", "col"), pairs(move))


def where_am_i():
    row = lax.axis_index("row")
    col = lax.axis_index("col")
    return row // 2, row % 2, col // X, col % X


def keep(count, start, rows):
    ids = lax.broadcasted_iota(jnp.int32, (rows, BLK), 0) + start
    return ids < count


def pack_kernel(map_ref, count_ref, gen_ref, diag_ref, coup_ref, loc_ref, rem_ref, send_ref, col_ref):
    y, k, z, x = where_am_i()
    zero = jnp.zeros((), jnp.bfloat16)
    loc_ref[...] = jnp.zeros_like(loc_ref)
    rem_ref[...] = jnp.zeros_like(rem_ref)
    send_ref[...] = jnp.zeros_like(send_ref)
    col_ref[...] = jnp.zeros_like(col_ref)
    t = z * X + x

    def one(i, carry):
        w = map_ref[k, y * CG + i] - y * WIN
        count = count_ref[k, y * CG + i]
        mine = lax.rem(w, 2) == k
        j = w // 2
        m = j // 4
        step = lax.rem(lax.rem(j, 4) - y + 4, 4)

        @pl.when(step == 0)
        def _():
            full = jnp.where(keep(count, 0, BLK), gen_ref[i], zero)

            @pl.when(mine)
            def _():
                loc_ref[m] = full

            @pl.when(jnp.logical_not(mine))
            def _():
                for part in range(4):
                    send_ref[6 + 4 * m + part] = full[64 * part : 64 * part + 64]

        @pl.when(step > 0)
        def _():
            parts = []
            for start in (QUART * x, BLK // 2 + QUART * z):
                start = pl.multiple_of(start, QUART)
                piece = gen_ref[i, pl.ds(start, QUART), :]
                parts.append(jnp.where(keep(count, start, QUART), piece, zero))

            @pl.when(mine)
            def _():
                rem_ref[step - 1, 0, m] = parts[0]
                rem_ref[step - 1, 1, m] = parts[1]

            @pl.when(jnp.logical_not(mine))
            def _():
                send_ref[2 * (step - 1) + m, :QUART] = parts[0]
                send_ref[2 * (step - 1) + m, QUART:] = parts[1]

        @pl.when(w == t)
        def _():
            full = jnp.where(keep(count, 0, BLK), gen_ref[i], zero)
            col_ref[0] = lax.dot_general(
                coup_ref[k], full, (((0,), (1,)), ((), ())), preferred_element_type=jnp.float32
            ).astype(jnp.bfloat16)
            lanes = lax.broadcasted_iota(jnp.int32, (BLK, BLK), 1) < count
            col_ref[1] = jnp.where(keep(count, 0, BLK) & lanes, diag_ref[i], zero)

        return carry

    lax.fori_loop(0, CG, one, 0)


def join_kernel(
    par_ref, loc_ref, swap_ref, r1, r2, r3, x1, x2, x3, z1, z2, z3,
    c0, c1, c2, c3, d0, d1, d2, d3, out_ref, rows_ref, cols_ref,
):
    y, k, z, x = where_am_i()
    a = pl.program_id(0)
    own = (c0, c1, c2, c3)
    other = (d0, d1, d2, d3)

    @pl.when(a == 0)
    def _():
        for m in range(2):
            rows_ref[2 * y + m, :, :BLK] = loc_ref[m]
            for part in range(4):
                rows_ref[2 * y + m, 64 * part : 64 * part + 64, BLK:] = swap_ref[6 + 4 * m + part]
        for step, got in ((1, r1), (2, r2), (3, r3)):
            s = lax.rem(y - step + 4, 4)
            for child in range(2):
                for m in range(2):
                    lanes = slice(BLK * child, BLK * child + BLK)
                    b = 2 * child + m
                    at = pl.multiple_of(QUART * x, QUART)
                    rows_ref[2 * s + m, pl.ds(at, QUART), lanes] = got[0, b]
                    at = pl.multiple_of(BLK // 2 + QUART * z, QUART)
                    rows_ref[2 * s + m, pl.ds(at, QUART), lanes] = got[1, b]
                    for far, gx, gz in ((1, x1, z1), (2, x2, z2), (3, x3, z3)):
                        at = pl.multiple_of(QUART * lax.rem(x - far + 4, 4), QUART)
                        rows_ref[2 * s + m, pl.ds(at, QUART), lanes] = gx[step - 1, b]
                        at = pl.multiple_of(BLK // 2 + QUART * lax.rem(z - far + 4, 4), QUART)
                        rows_ref[2 * s + m, pl.ds(at, QUART), lanes] = gz[step - 1, b]
        for step in range(4):
            s = lax.rem(y - step + 4, 4)
            cols_ref[s, :BLK] = own[step][0]
            cols_ref[s, BLK:] = other[step][0]

    left = rows_ref[a]
    for b in range(4):
        tile = jnp.dot(left, cols_ref[b], preferred_element_type=jnp.float32)
        for half in range(2):
            at = pl.ds(4 * half + b, BLK, stride=8)
            out_ref[0, at, :] = par_ref[0, at, :] + tile[:, 128 * half : 128 * half + 128]

    t = z * X + x
    row = 2 * y + k

    @pl.when((row == lax.rem(t, 8)) & (lax.rem(a, 2) == t // 8))
    def _():
        for step in range(4):

            @pl.when(lax.rem(y - step + 4, 4) == a // 2)
            def _():
                both = own[step][1].astype(jnp.float32) + other[step][1].astype(jnp.float32)
                for half in range(2):
                    at = pl.ds(4 * half + a // 2, BLK, stride=8)
                    out_ref[0, at, :] = out_ref[0, at, :] + both[:, 128 * half : 128 * half + 128]


def shards(parent_front, generators, diagonal_blocks, coupling, block_map, valid_rows):
    bf16 = jnp.bfloat16
    vmem = pl.BlockSpec(memory_space=pltpu.VMEM)
    smem = pl.BlockSpec(memory_space=pltpu.SMEM)
    loc, rem, send, col = pl.pallas_call(
        pack_kernel,
        out_shape=(
            jax.ShapeDtypeStruct((2, BLK, BLK), bf16),
            jax.ShapeDtypeStruct((3, 2, 2, QUART, BLK), bf16),
            jax.ShapeDtypeStruct((14, 2 * QUART, BLK), bf16),
            jax.ShapeDtypeStruct((2, BLK, BLK), bf16),
        ),
        in_specs=[smem, smem, vmem, vmem, vmem],
        out_specs=(vmem, vmem, vmem, vmem),
        compiler_params=pltpu.CompilerParams(vmem_limit_bytes=16 * 2**20),
    )(block_map, valid_rows, generators, diagonal_blocks, coupling)

    flip = lambda y, k, z, x: (y, 1 - k, z, x)
    swap = shift(send, flip)
    got = []
    for step in (1, 3, 2):
        there = swap[2 * step - 2 : 2 * step].reshape(2, 2, QUART, BLK).swapaxes(0, 1)
        payload = jnp.concatenate([rem[step - 1], there], axis=1)
        got.append(shift(payload, lambda y, k, z, x, n=step: (y + n, k, z, x)))
    got = [got[0], got[2], got[1]]
    cols = [col] + [shift(col, lambda y, k, z, x, n=step: (y + n, k, z, x)) for step in (1, 2, 3)]
    others = [shift(c, flip) for c in cols]
    for_x = jnp.stack([g[0] for g in got])
    for_z = jnp.stack([g[1] for g in got])
    xs = [shift(for_x, lambda y, k, z, x, n=far: (y, k, z, x + n)) for far in (1, 2, 3)]
    zs = [shift(for_z, lambda y, k, z, x, n=far: (y, k, z + n, x)) for far in (1, 2, 3)]

    a_count = parent_front.shape[0]
    flat = parent_front.reshape(a_count, BLK, 4, 2, 128).transpose(0, 1, 3, 2, 4).reshape(a_count, BLK * 8, 128)
    block = pl.BlockSpec((1, BLK * 8, 128), lambda a: (a, 0, 0))
    joined = pl.pallas_call(
        join_kernel,
        grid=(a_count,),
        out_shape=jax.ShapeDtypeStruct(flat.shape, jnp.float32),
        in_specs=[block] + [vmem] * 19,
        out_specs=block,
        scratch_shapes=[
            pltpu.VMEM((a_count, BLK, 2 * BLK), bf16),
            pltpu.VMEM((4, 2 * BLK, BLK), bf16),
        ],
        compiler_params=pltpu.CompilerParams(vmem_limit_bytes=32 * 2**20),
    )(flat, loc, swap, *got, *xs, *zs, *cols, *others)
    return joined.reshape(a_count, BLK, 2, 4, 128).transpose(0, 1, 3, 2, 4).reshape(parent_front.shape)


def solution(mesh):
    in_specs = (P(None, "row", None, "col"), P("row", None, None), P("row", None, None), P(), P(), P())
    out_specs = P(None, "row", None, "col")
    return jax.shard_map(shards, mesh=mesh, in_specs=in_specs, out_specs=out_specs, check_vma=False)
```

time: 95 us -> 73.2 us (0.77)
  between operations: 13.5 us -> 0.13 us
  other arithmetic: 12.2 us -> 0.1 us
  starting transfers between devices: 4.58 us -> 16.1 us
  matrix products: 10.1 us -> 0 us
  local copies, waits for them, and re-layouts: 18.4 us -> 8.58 us
  Pallas kernels: 0 us -> 8.88 us
  waiting for transfers between devices: 35.5 us -> 39.2 us
    ppermute x0 -> x17, waiting for transfers between devices: none -> 39.2 us  [shift(): return lax.ppermute(value, ('row', 'col'), pairs(move))]
    all_to_all x1 -> x0, waiting for transfers between devices: 35.5 us -> none  [shards(): lax.all_to_all(row_send, 'row', split_axis=0, concat_axis=0, tiled=True)]
    ppermute x0 -> x17, starting transfers between devices: none -> 16.1 us  [shift(): return lax.ppermute(value, ('row', 'col'), pairs(move))]
    add x1 -> x0, local copies, waits for them, and re-layouts: 12.2 us -> none  [shards(): running = running + rounded.astype(jnp.float32)]
    add x3 -> x0, other arithmetic: 10.5 us -> none  [the longest x1 10.5 us: shards(): running = running + rounded.astype(jnp.float32)]
    dot_general x6 -> x0, matrix products: 10.1 us -> none  [the longest x2 4.84 us: shards(): jnp.einsum('axq,bzq->axbz', row_received[child_index], col_received[child...]
    pallas_call x0 -> x2, Pallas kernels: none -> 8.88 us  [the longest x1 7.35 us: shards(): pl.pallas_call(join_kernel, grid=(a_count,), out_shape=jax.ShapeDtypeStru...]
    unnamed x8 -> x12, local copies, waits for them, and re-layouts: 0.07 us -> 8.5 us
  transfers between devices with their start and end apart: 2 -> 17, of which waited for: 1 -> 10; matrix products, arithmetic and copies ran while one was open for 5% -> 0% of each run, Pallas kernels for 0% -> 0%
where the time goes in v1:
time: 73.2 us; the launch traced here: 72.9 us
  waiting for transfers between devices  39.2 us (54%)
  starting transfers between devices  16.1 us (22%)
  Pallas kernels  8.88 us (12%)
  local copies, waits for them, and re-layouts  8.58 us (12%)
    ppermute x17, waiting for transfers between devices, shift(): return lax.ppermute(value, ('row', 'col'), pairs(move))  39.2 us
    ppermute x17, starting transfers between devices, shift(): return lax.ppermute(value, ('row', 'col'), pairs(move))  16.1 us
    unnamed x12, local copies, waits for them, and re-layouts  8.5 us
    pallas_call x1, Pallas kernels, shards(): pl.pallas_call(join_kernel, grid=(a_count,), out_shape=jax.ShapeDtypeStru...  7.35 us
    pallas_call x1, Pallas kernels, shards(): pl.pallas_call(pack_kernel, out_shape=(jax.ShapeDtypeStruct((2, BLK, BLK)...  1.53 us
  transfers between devices with their start and end apart: 17, of which 10 were waited for; matrix products, arithmetic and copies ran while one was open for 0% of the time, Pallas kernels for 0%

profile of v1, /device:TPU:0, one launch (start us, length us, event | category | flops | bytes accessed | tf_op | source)
XLA Modules:
  0.0 72.9 jit_solution(9311965269647627519)
XLA Ops:
  0.0 0.0 copy-start.1
  0.0 1.4 %copy-done.1 = bf16[12,256,256]{2,1,0:T(8,128)(2,1)S(1)} copy-done((bf16[12,256,256]{2,1,0:T(8,128)(2,1)S(1)}, bf16[12,256,256]{2,1,0:T(8,128)(2,1)}, u32[]{:S(2)}) %copy-start.1) | copy-done | bytes 1572888
  1.4 0.0 copy-start.2
  1.4 1.4 %copy-done.2 = bf16[12,256,256]{2,1,0:T(8,128)(2,1)S(1)} copy-done((bf16[12,256,256]{2,1,0:T(8,128)(2,1)S(1)}, bf16[12,256,256]{2,1,0:T(8,128)(2,1)}, u32[]{:S(2)}) %copy-start.2) | copy-done | bytes 1572888
  2.8 0.0 copy-start.3
  2.8 0.9 %copy-done.3 = bf16[2,256,256]{2,1,0:T(8,128)(2,1)S(1)} copy-done((bf16[2,256,256]{2,1,0:T(8,128)(2,1)S(1)}, bf16[2,256,256]{2,1,0:T(8,128)(2,1)}, u32[]{:S(2)}) %copy-start.3) | copy-done | bytes 262168
  3.8 0.0 copy-start.4
  3.8 0.7 copy-done.4
  4.4 0.0 copy-start.5
  4.4 0.7 copy-done.5
  5.1 1.5 %shard_map.64 = (bf16[2,256,256]{2,1,0:T(8,128)(2,1)S(1)}, bf16[3,2,2,32,256]{4,3,2,1,0:T(8,128)(2,1)S(1)}, bf16[14,64,256]{2,1,0:T(8,128)(2,1)S(1)}, bf16[2,256,256]{2,1,0:T(8,128)(2,1)S(1)}) custom-call(s32[2,48]{1,0:T(2,128)S(1)} %copy-done.4, s32[2,48]{1,0:T(2,128)S(1)} %copy-done.5, bf16[12,256,256]{2,1,0:T(8,128)(2,1)S(1)} %copy-done.1, ...), custom_call_target="tpu_custom_call" | custom-call | tf_op jit(solution)/shard_map/pallas_call | solution.py:166
  6.7 0.1 collective-permute-start
  6.8 3.2 %collective-permute-start.12 = (bf16[2,256,256]{2,1,0:T(8,128)(2,1)S(1)}, bf16[2,256,256]{2,1,0:T(8,128)(2,1)S(1)}, u32[]{:S(2)}, u32[]{:S(2)}) collective-permute-start(bf16[2,256,256]{2,1,0:T(8,128)(2,1)S(1)} %get-tuple-element.12.c0), channel_id=1, source_target_pairs={{0,96},{1,97},{2,98},{3,99},{4,100},{5,101},{6,102},{7,103},{8,104... | collective-permute-start | bytes 786440 | tf_op jit(solution)/shard_map/ppermute | solution.py:29
  9.9 0.6 collective-permute-start.11
  10.6 1.0 %collective-permute-start.10 = (bf16[2,256,256]{2,1,0:T(8,128)(2,1)S(1)}, bf16[2,256,256]{2,1,0:T(8,128)(2,1)S(1)}, u32[]{:S(2)}, u32[]{:S(2)}) collective-permute-start(bf16[2,256,256]{2,1,0:T(8,128)(2,1)S(1)} %get-tuple-element.12.c0), channel_id=1, source_target_pairs={{0,32},{1,33},{2,34},{3,35},{4,36},{5,37},{6,38},{7,39},{8,40},{9,... | collective-permute-start | bytes 786440 | tf_op jit(solution)/shard_map/ppermute | solution.py:29
  11.6 0.0 collective-permute-start.13
  11.6 10.1 %collective-permute-done.12.c3 = bf16[2,256,256]{2,1,0:T(8,128)(2,1)S(1)} collective-permute-done((bf16[2,256,256]{2,1,0:T(8,128)(2,1)S(1)}, bf16[2,256,256]{2,1,0:T(8,128)(2,1)S(1)}, u32[]{:S(2)}, u32[]{:S(2)}) %collective-permute-start.12) | collective-permute-done | bytes 262176 | tf_op jit(solution)/shard_map/ppermute | solution.py:29
  21.7 0.0 collective-permute-start.16
  21.7 0.0 collective-permute-done.11.c2
  21.7 0.5 collective-permute-start.15
  22.2 3.2 %collective-permute-done.10.c1 = bf16[2,256,256]{2,1,0:T(8,128)(2,1)S(1)} collective-permute-done((bf16[2,256,256]{2,1,0:T(8,128)(2,1)S(1)}, bf16[2,256,256]{2,1,0:T(8,128)(2,1)S(1)}, u32[]{:S(2)}, u32[]{:S(2)}) %collective-permute-start.10) | collective-permute-done | bytes 262176 | tf_op jit(solution)/shard_map/ppermute | solution.py:29
  25.4 0.0 collective-permute-start.14
  25.4 0.0 collective-permute-done.swap_ref
  25.5 0.1 collective-permute-start.1
  25.7 7.0 %collective-permute-done.1.r1 = bf16[2,4,32,256]{3,2,1,0:T(8,128)(2,1)S(1)} collective-permute-done((bf16[2,4,32,256]{3,2,1,0:T(8,128)(2,1)S(1)}, bf16[2,4,32,256]{3,2,1,0:T(8,128)(2,1)S(1)}, u32[]{:S(2)}, u32[]{:S(2)}) %collective-permute-start.1) | collective-permute-done | bytes 131104 | tf_op jit(solution)/shard_map/ppermute | solution.py:29
  32.7 0.0 collective-permute-start.2
  32.7 6.5 %collective-permute-done.2.r2 = bf16[2,4,32,256]{3,2,1,0:T(8,128)(2,1)S(1)} collective-permute-done((bf16[2,4,32,256]{3,2,1,0:T(8,128)(2,1)S(1)}, bf16[2,4,32,256]{3,2,1,0:T(8,128)(2,1)S(1)}, u32[]{:S(2)}, u32[]{:S(2)}) %collective-permute-start.2) | collective-permute-done | bytes 131104 | tf_op jit(solution)/shard_map/ppermute | solution.py:29
  39.2 0.0 collective-permute-start.3
  39.3 5.0 %collective-permute-done.3.r3 = bf16[2,4,32,256]{3,2,1,0:T(8,128)(2,1)S(1)} collective-permute-done((bf16[2,4,32,256]{3,2,1,0:T(8,128)(2,1)S(1)}, bf16[2,4,32,256]{3,2,1,0:T(8,128)(2,1)S(1)}, u32[]{:S(2)}, u32[]{:S(2)}) %collective-permute-start.3) | collective-permute-done | bytes 131104 | tf_op jit(solution)/shard_map/ppermute | solution.py:29
  44.3 2.7 %collective-permute-start.6 = (bf16[3,4,32,256]{3,2,1,0:T(8,128)(2,1)S(1)}, bf16[3,4,32,256]{3,2,1,0:T(8,128)(2,1)S(1)}, u32[]{:S(2)}, u32[]{:S(2)}) collective-permute-start(bf16[3,4,32,256]{3,2,1,0:T(8,128)(2,1)S(1)} %pad_maximum_fusion), channel_id=1, source_target_pairs={{0,3},{1,0},{2,1},{3,2},{4,7},{5,4},{6,5},{7,6},{8,11},{9,8},{10,9... | collective-permute-start | bytes 589832 | tf_op jit(solution)/shard_map/ppermute | solution.py:29
  47.0 0.0 collective-permute-done.13.d0
  47.0 0.8 %collective-permute-start.5 = (bf16[3,4,32,256]{3,2,1,0:T(8,128)(2,1)S(1)}, bf16[3,4,32,256]{3,2,1,0:T(8,128)(2,1)S(1)}, u32[]{:S(2)}, u32[]{:S(2)}) collective-permute-start(bf16[3,4,32,256]{3,2,1,0:T(8,128)(2,1)S(1)} %pad_maximum_fusion), channel_id=1, source_target_pairs={{0,2},{1,3},{2,0},{3,1},{4,6},{5,7},{6,4},{7,5},{8,10},{9,11},{10,... | collective-permute-start | bytes 589832 | tf_op jit(solution)/shard_map/ppermute | solution.py:29
  47.8 0.0 collective-permute-done.16.d3
  47.8 1.1 %collective-permute-start.4 = (bf16[3,4,32,256]{3,2,1,0:T(8,128)(2,1)S(1)}, bf16[3,4,32,256]{3,2,1,0:T(8,128)(2,1)S(1)}, u32[]{:S(2)}, u32[]{:S(2)}) collective-permute-start(bf16[3,4,32,256]{3,2,1,0:T(8,128)(2,1)S(1)} %pad_maximum_fusion), channel_id=1, source_target_pairs={{0,1},{1,2},{2,3},{3,0},{4,5},{5,6},{6,7},{7,4},{8,9},{9,10},{10,1... | collective-permute-start | bytes 589832 | tf_op jit(solution)/shard_map/ppermute | solution.py:29
  48.9 0.0 collective-permute-done.15.d2
  48.9 4.0 %collective-permute-start.9 = (bf16[3,4,32,256]{3,2,1,0:T(8,128)(2,1)S(1)}, bf16[3,4,32,256]{3,2,1,0:T(8,128)(2,1)S(1)}, u32[]{:S(2)}, u32[]{:S(2)}) collective-permute-start(bf16[3,4,32,256]{3,2,1,0:T(8,128)(2,1)S(1)} %pad_maximum_fusion.1), channel_id=1, source_target_pairs={{0,12},{1,13},{2,14},{3,15},{4,0},{5,1},{6,2},{7,3},{8,4},{9,5},{1... | collective-permute-start | bytes 589832 | tf_op jit(solution)/shard_map/ppermute | solution.py:29
  52.9 0.0 collective-permute-done.14.d1
  52.9 0.0 collective-permute-start.8
  52.9 0.2 collective-permute-done.6.x3
  53.2 2.0 %collective-permute-start.7 = (bf16[3,4,32,256]{3,2,1,0:T(8,128)(2,1)S(1)}, bf16[3,4,32,256]{3,2,1,0:T(8,128)(2,1)S(1)}, u32[]{:S(2)}, u32[]{:S(2)}) collective-permute-start(bf16[3,4,32,256]{3,2,1,0:T(8,128)(2,1)S(1)} %pad_maximum_fusion.1), channel_id=1, source_target_pairs={{0,4},{1,5},{2,6},{3,7},{4,8},{5,9},{6,10},{7,11},{8,12},{9,13},{1... | collective-permute-start | bytes 589832 | tf_op jit(solution)/shard_map/ppermute | solution.py:29
  55.1 0.0 collective-permute-done.5.x2
  55.1 1.8 %collective-permute-done.4.x1 = bf16[3,4,32,256]{3,2,1,0:T(8,128)(2,1)S(1)} collective-permute-done((bf16[3,4,32,256]{3,2,1,0:T(8,128)(2,1)S(1)}, bf16[3,4,32,256]{3,2,1,0:T(8,128)(2,1)S(1)}, u32[]{:S(2)}, u32[]{:S(2)}) %collective-permute-start.4) | collective-permute-done | bytes 196640 | tf_op jit(solution)/shard_map/ppermute | solution.py:29
  56.9 1.3 %collective-permute-done.9.z3 = bf16[3,4,32,256]{3,2,1,0:T(8,128)(2,1)S(1)} collective-permute-done((bf16[3,4,32,256]{3,2,1,0:T(8,128)(2,1)S(1)}, bf16[3,4,32,256]{3,2,1,0:T(8,128)(2,1)S(1)}, u32[]{:S(2)}, u32[]{:S(2)}) %collective-permute-start.9) | collective-permute-done | bytes 196640 | tf_op jit(solution)/shard_map/ppermute | solution.py:29
  58.3 1.9 %collective-permute-done.8.z2 = bf16[3,4,32,256]{3,2,1,0:T(8,128)(2,1)S(1)} collective-permute-done((bf16[3,4,32,256]{3,2,1,0:T(8,128)(2,1)S(1)}, bf16[3,4,32,256]{3,2,1,0:T(8,128)(2,1)S(1)}, u32[]{:S(2)}, u32[]{:S(2)}) %collective-permute-start.8) | collective-permute-done | bytes 196640 | tf_op jit(solution)/shard_map/ppermute | solution.py:29
  60.2 2.0 %collective-permute-done.7.z1 = bf16[3,4,32,256]{3,2,1,0:T(8,128)(2,1)S(1)} collective-permute-done((bf16[3,4,32,256]{3,2,1,0:T(8,128)(2,1)S(1)}, bf16[3,4,32,256]{3,2,1,0:T(8,128)(2,1)S(1)}, u32[]{:S(2)}, u32[]{:S(2)}) %collective-permute-start.7) | collective-permute-done | bytes 196640 | tf_op jit(solution)/shard_map/ppermute | solution.py:29
  62.2 0.0 copy-start
  62.2 3.4 %copy-done = f32[8,256,4,256]{3,2,1,0:T(4,128)S(1)} copy-done((f32[8,256,4,256]{3,2,1,0:T(4,128)S(1)}, f32[8,256,4,256]{3,2,1,0:T(4,128)}, u32[]{:S(2)}) %copy-start) | copy-done | bytes 8388632
  65.6 7.3 %shard_map.65 = f32[8,2048,128]{2,1,0:T(8,128)} custom-call(f32[8,2048,128]{2,1,0:T(8,128)S(1)} %bitcast.28, bf16[2,256,256]{2,1,0:T(8,128)(2,1)S(1)} %get-tuple-element.9.loc_ref, bf16[14,64,256]{2,1,0:T(8,128)(2,1)S(1)} %collective-permute-done.swap_ref, bf16[2,4,32,256]{3,2,1,0:T(8,128)(2,1)S(1)} %collective-permute-done.1.r1, ...), custom_call_target="tpu_custom_call" | custom-call | tf_op jit(solution)/shard_map/pallas_call | solution.py:197
  (13 shorter events, 0.2 us)
Async XLA Ops:
  0.0 1.4 %copy-start.1 = (bf16[12,256,256]{2,1,0:T(8,128)(2,1)S(1)}, bf16[12,256,256]{2,1,0:T(8,128)(2,1)}, u32[]{:S(2)}) copy-start(bf16[12,256,256]{2,1,0:T(8,128)(2,1)} %gen_ref.1) | copy-start | bytes 4718596
  1.4 1.4 %copy-start.2 = (bf16[12,256,256]{2,1,0:T(8,128)(2,1)S(1)}, bf16[12,256,256]{2,1,0:T(8,128)(2,1)}, u32[]{:S(2)}) copy-start(bf16[12,256,256]{2,1,0:T(8,128)(2,1)} %diag_ref.1) | copy-start | bytes 4718596
  2.8 0.9 %copy-start.3 = (bf16[2,256,256]{2,1,0:T(8,128)(2,1)S(1)}, bf16[2,256,256]{2,1,0:T(8,128)(2,1)}, u32[]{:S(2)}) copy-start(bf16[2,256,256]{2,1,0:T(8,128)(2,1)} %coup_ref.1) | copy-start | bytes 786436
  3.8 0.7 copy-start.4
  4.4 0.7 copy-start.5
  6.7 18.8 %collective-permute-start = (bf16[14,64,256]{2,1,0:T(8,128)(2,1)S(1)}, bf16[14,64,256]{2,1,0:T(8,128)(2,1)S(1)}, u32[]{:S(2)}, u32[]{:S(2)}) collective-permute-start(bf16[14,64,256]{2,1,0:T(8,128)(2,1)S(1)} %get-tuple-element.10), channel_id=1, source_target_pairs={{0,16},{1,17},{2,18},{3,19},{4,20},{5,21},{6,22},{7,23},{8,24},{9,... | collective-permute-start | bytes 1376264 | tf_op jit(solution)/shard_map/ppermute | solution.py:29
  6.8 15.0 %collective-permute-start.12 = (bf16[2,256,256]{2,1,0:T(8,128)(2,1)S(1)}, bf16[2,256,256]{2,1,0:T(8,128)(2,1)S(1)}, u32[]{:S(2)}, u32[]{:S(2)}) collective-permute-start(bf16[2,256,256]{2,1,0:T(8,128)(2,1)S(1)} %get-tuple-element.12.c0), channel_id=1, source_target_pairs={{0,96},{1,97},{2,98},{3,99},{4,100},{5,101},{6,102},{7,103},{8,104... | collective-permute-start | bytes 786440 | tf_op jit(solution)/shard_map/ppermute | solution.py:29
  9.9 11.8 %collective-permute-start.11 = (bf16[2,256,256]{2,1,0:T(8,128)(2,1)S(1)}, bf16[2,256,256]{2,1,0:T(8,128)(2,1)S(1)}, u32[]{:S(2)}, u32[]{:S(2)}) collective-permute-start(bf16[2,256,256]{2,1,0:T(8,128)(2,1)S(1)} %get-tuple-element.12.c0), channel_id=1, source_target_pairs={{0,64},{1,65},{2,66},{3,67},{4,68},{5,69},{6,70},{7,71},{8,72},{9,... | collective-permute-start | bytes 786440 | tf_op jit(solution)/shard_map/ppermute | solution.py:29
  10.6 14.8 %collective-permute-start.10 = (bf16[2,256,256]{2,1,0:T(8,128)(2,1)S(1)}, bf16[2,256,256]{2,1,0:T(8,128)(2,1)S(1)}, u32[]{:S(2)}, u32[]{:S(2)}) collective-permute-start(bf16[2,256,256]{2,1,0:T(8,128)(2,1)S(1)} %get-tuple-element.12.c0), channel_id=1, source_target_pairs={{0,32},{1,33},{2,34},{3,35},{4,36},{5,37},{6,38},{7,39},{8,40},{9,... | collective-permute-start | bytes 786440 | tf_op jit(solution)/shard_map/ppermute | solution.py:29
  11.6 35.4 %collective-permute-start.13 = (bf16[2,256,256]{2,1,0:T(8,128)(2,1)S(1)}, bf16[2,256,256]{2,1,0:T(8,128)(2,1)S(1)}, u32[]{:S(2)}, u32[]{:S(2)}) collective-permute-start(bf16[2,256,256]{2,1,0:T(8,128)(2,1)S(1)} %get-tuple-element.12.c0), channel_id=1, source_target_pairs={{0,16},{1,17},{2,18},{3,19},{4,20},{5,21},{6,22},{7,23},{8,24},{9,... | collective-permute-start | bytes 786440 | tf_op jit(solution)/shard_map/ppermute | solution.py:29
  21.7 26.1 %collective-permute-start.16 = (bf16[2,256,256]{2,1,0:T(8,128)(2,1)S(1)}, bf16[2,256,256]{2,1,0:T(8,128)(2,1)S(1)}, u32[]{:S(2)}, u32[]{:S(2)}) collective-permute-start(bf16[2,256,256]{2,1,0:T(8,128)(2,1)S(1)} %collective-permute-done.12.c3), channel_id=1, source_target_pairs={{0,16},{1,17},{2,18},{3,19},{4,20},{5,21},{6,22},{7,23},{8,24},{9,... | collective-permute-start | bytes 786440 | tf_op jit(solution)/shard_map/ppermute | solution.py:29
  21.7 27.2 %collective-permute-start.15 = (bf16[2,256,256]{2,1,0:T(8,128)(2,1)S(1)}, bf16[2,256,256]{2,1,0:T(8,128)(2,1)S(1)}, u32[]{:S(2)}, u32[]{:S(2)}) collective-permute-start(bf16[2,256,256]{2,1,0:T(8,128)(2,1)S(1)} %collective-permute-done.11.c2), channel_id=1, source_target_pairs={{0,16},{1,17},{2,18},{3,19},{4,20},{5,21},{6,22},{7,23},{8,24},{9,... | collective-permute-start | bytes 786440 | tf_op jit(solution)/shard_map/ppermute | solution.py:29
  25.4 27.5 %collective-permute-start.14 = (bf16[2,256,256]{2,1,0:T(8,128)(2,1)S(1)}, bf16[2,256,256]{2,1,0:T(8,128)(2,1)S(1)}, u32[]{:S(2)}, u32[]{:S(2)}) collective-permute-start(bf16[2,256,256]{2,1,0:T(8,128)(2,1)S(1)} %collective-permute-done.10.c1), channel_id=1, source_target_pairs={{0,16},{1,17},{2,18},{3,19},{4,20},{5,21},{6,22},{7,23},{8,24},{9,... | collective-permute-start | bytes 786440 | tf_op jit(solution)/shard_map/ppermute | solution.py:29
  25.5 7.2 %collective-permute-start.1 = (bf16[2,4,32,256]{3,2,1,0:T(8,128)(2,1)S(1)}, bf16[2,4,32,256]{3,2,1,0:T(8,128)(2,1)S(1)}, u32[]{:S(2)}, u32[]{:S(2)}) collective-permute-start(bf16[2,4,32,256]{3,2,1,0:T(8,128)(2,1)S(1)} %pad_maximum_fusion.2), channel_id=1, source_target_pairs={{0,32},{1,33},{2,34},{3,35},{4,36},{5,37},{6,38},{7,39},{8,40},{9,... | collective-permute-start | bytes 393224 | tf_op jit(solution)/shard_map/ppermute | solution.py:29
  32.7 6.5 %collective-permute-start.2 = (bf16[2,4,32,256]{3,2,1,0:T(8,128)(2,1)S(1)}, bf16[2,4,32,256]{3,2,1,0:T(8,128)(2,1)S(1)}, u32[]{:S(2)}, u32[]{:S(2)}) collective-permute-start(bf16[2,4,32,256]{3,2,1,0:T(8,128)(2,1)S(1)} %pad_maximum_fusion.3), channel_id=1, source_target_pairs={{0,64},{1,65},{2,66},{3,67},{4,68},{5,69},{6,70},{7,71},{8,72},{9,... | collective-permute-start | bytes 393224 | tf_op jit(solution)/shard_map/ppermute | solution.py:29
  39.2 5.0 %collective-permute-start.3 = (bf16[2,4,32,256]{3,2,1,0:T(8,128)(2,1)S(1)}, bf16[2,4,32,256]{3,2,1,0:T(8,128)(2,1)S(1)}, u32[]{:S(2)}, u32[]{:S(2)}) collective-permute-start(bf16[2,4,32,256]{3,2,1,0:T(8,128)(2,1)S(1)} %pad_maximum_fusion.4), channel_id=1, source_target_pairs={{0,96},{1,97},{2,98},{3,99},{4,100},{5,101},{6,102},{7,103},{8,104... | collective-permute-start | bytes 393224 | tf_op jit(solution)/shard_map/ppermute | solution.py:29
  44.3 8.9 %collective-permute-start.6 = (bf16[3,4,32,256]{3,2,1,0:T(8,128)(2,1)S(1)}, bf16[3,4,32,256]{3,2,1,0:T(8,128)(2,1)S(1)}, u32[]{:S(2)}, u32[]{:S(2)}) collective-permute-start(bf16[3,4,32,256]{3,2,1,0:T(8,128)(2,1)S(1)} %pad_maximum_fusion), channel_id=1, source_target_pairs={{0,3},{1,0},{2,1},{3,2},{4,7},{5,4},{6,5},{7,6},{8,11},{9,8},{10,9... | collective-permute-start | bytes 589832 | tf_op jit(solution)/shard_map/ppermute | solution.py:29
  47.0 8.2 %collective-permute-start.5 = (bf16[3,4,32,256]{3,2,1,0:T(8,128)(2,1)S(1)}, bf16[3,4,32,256]{3,2,1,0:T(8,128)(2,1)S(1)}, u32[]{:S(2)}, u32[]{:S(2)}) collective-permute-start(bf16[3,4,32,256]{3,2,1,0:T(8,128)(2,1)S(1)} %pad_maximum_fusion), channel_id=1, source_target_pairs={{0,2},{1,3},{2,0},{3,1},{4,6},{5,7},{6,4},{7,5},{8,10},{9,11},{10,... | collective-permute-start | bytes 589832 | tf_op jit(solution)/shard_map/ppermute | solution.py:29
  47.8 9.2 %collective-permute-start.4 = (bf16[3,4,32,256]{3,2,1,0:T(8,128)(2,1)S(1)}, bf16[3,4,32,256]{3,2,1,0:T(8,128)(2,1)S(1)}, u32[]{:S(2)}, u32[]{:S(2)}) collective-permute-start(bf16[3,4,32,256]{3,2,1,0:T(8,128)(2,1)S(1)} %pad_maximum_fusion), channel_id=1, source_target_pairs={{0,1},{1,2},{2,3},{3,0},{4,5},{5,6},{6,7},{7,4},{8,9},{9,10},{10,1... | collective-permute-start | bytes 589832 | tf_op jit(solution)/shard_map/ppermute | solution.py:29
  48.9 9.4 %collective-permute-start.9 = (bf16[3,4,32,256]{3,2,1,0:T(8,128)(2,1)S(1)}, bf16[3,4,32,256]{3,2,1,0:T(8,128)(2,1)S(1)}, u32[]{:S(2)}, u32[]{:S(2)}) collective-permute-start(bf16[3,4,32,256]{3,2,1,0:T(8,128)(2,1)S(1)} %pad_maximum_fusion.1), channel_id=1, source_target_pairs={{0,12},{1,13},{2,14},{3,15},{4,0},{5,1},{6,2},{7,3},{8,4},{9,5},{1... | collective-permute-start | bytes 589832 | tf_op jit(solution)/shard_map/ppermute | solution.py:29
  52.9 7.3 %collective-permute-start.8 = (bf16[3,4,32,256]{3,2,1,0:T(8,128)(2,1)S(1)}, bf16[3,4,32,256]{3,2,1,0:T(8,128)(2,1)S(1)}, u32[]{:S(2)}, u32[]{:S(2)}) collective-permute-start(bf16[3,4,32,256]{3,2,1,0:T(8,128)(2,1)S(1)} %pad_maximum_fusion.1), channel_id=1, source_target_pairs={{0,8},{1,9},{2,10},{3,11},{4,12},{5,13},{6,14},{7,15},{8,0},{9,1},... | collective-permute-start | bytes 589832 | tf_op jit(solution)/shard_map/ppermute | solution.py:29
  53.2 9.1 %collective-permute-start.7 = (bf16[3,4,32,256]{3,2,1,0:T(8,128)(2,1)S(1)}, bf16[3,4,32,256]{3,2,1,0:T(8,128)(2,1)S(1)}, u32[]{:S(2)}, u32[]{:S(2)}) collective-permute-start(bf16[3,4,32,256]{3,2,1,0:T(8,128)(2,1)S(1)} %pad_maximum_fusion.1), channel_id=1, source_target_pairs={{0,4},{1,5},{2,6},{3,7},{4,8},{5,9},{6,10},{7,11},{8,12},{9,13},{1... | collective-permute-start | bytes 589832 | tf_op jit(solution)/shard_map/ppermute | solution.py:29
  62.2 3.4 %copy-start = (f32[8,256,4,256]{3,2,1,0:T(4,128)S(1)}, f32[8,256,4,256]{3,2,1,0:T(4,128)}, u32[]{:S(2)}) copy-start(f32[8,256,4,256]{3,2,1,0:T(4,128)} %param.6) | copy-start | bytes 25165828

commit v2 on v1

--- a/solution.py
+++ b/solution.py
@@ -1,11 +1,10 @@
-import functools
-
 import jax
 import jax.numpy as jnp
 from jax import lax
 from jax.experimental import pallas as pl
 from jax.experimental.pallas import tpu as pltpu
 from jax.sharding import PartitionSpec as P
+
 
 Y, Z, X, BLK = 4, 4, 4, 256
 QUART = BLK // 8
@@ -40,14 +39,21 @@
     return ids < count
 
 
-def pack_kernel(map_ref, count_ref, gen_ref, diag_ref, coup_ref, loc_ref, rem_ref, send_ref, col_ref):
+def rows_kernel(map_hbm, count_hbm, gen_hbm, loc_ref, rem_ref, send_ref, map_ref, count_ref, gen_ref, sems):
     y, k, z, x = where_am_i()
+    copies = [
+        pltpu.make_async_copy(map_hbm, map_ref, sems.at[0]),
+        pltpu.make_async_copy(count_hbm, count_ref, sems.at[1]),
+        pltpu.make_async_copy(gen_hbm, gen_ref, sems.at[2]),
+    ]
+    for copy in copies:
+        copy.start()
     zero = jnp.zeros((), jnp.bfloat16)
     loc_ref[...] = jnp.zeros_like(loc_ref)
     rem_ref[...] = jnp.zeros_like(rem_ref)
     send_ref[...] = jnp.zeros_like(send_ref)
-    col_ref[...] = jnp.zeros_like(col_ref)
-    t = z * X + x
+    for copy in copies:
+        copy.wait()
 
     def one(i, carry):
         w = map_ref[k, y * CG + i] - y * WIN
@@ -88,18 +94,53 @@
                 send_ref[2 * (step - 1) + m, :QUART] = parts[0]
                 send_ref[2 * (step - 1) + m, QUART:] = parts[1]
 
-        @pl.when(w == t)
-        def _():
-            full = jnp.where(keep(count, 0, BLK), gen_ref[i], zero)
-            col_ref[0] = lax.dot_general(
-                coup_ref[k], full, (((0,), (1,)), ((), ())), preferred_element_type=jnp.float32
-            ).astype(jnp.bfloat16)
-            lanes = lax.broadcasted_iota(jnp.int32, (BLK, BLK), 1) < count
-            col_ref[1] = jnp.where(keep(count, 0, BLK) & lanes, diag_ref[i], zero)
-
         return carry
 
     lax.fori_loop(0, CG, one, 0)
+
+
+def column_kernel(map_hbm, count_hbm, gen_hbm, diag_hbm, coup_hbm, col_ref, map_ref, count_ref, gen_ref, diag_ref, coup_ref, sems):
+    y, k, z, x = where_am_i()
+    target = y * WIN + z * X + x
+    coup = pltpu.make_async_copy(coup_hbm.at[k], coup_ref, sems.at[2])
+    coup.start()
+    tables = [
+        pltpu.make_async_copy(map_hbm, map_ref, sems.at[0]),
+        pltpu.make_async_copy(count_hbm, count_ref, sems.at[1]),
+    ]
+    for copy in tables:
+        copy.start()
+    for copy in tables:
+        copy.wait()
+    which = jnp.int32(0)
+    count = jnp.int32(0)
+    for i in range(CG):
+        hit = map_ref[k, y * CG + i] == target
+        which = jnp.where(hit, i, which)
+        count = jnp.where(hit, count_ref[k, y * CG + i], count)
+    blocks = [
+        pltpu.make_async_copy(gen_hbm.at[which], gen_ref, sems.at[3]),
+        pltpu.make_async_copy(diag_hbm.at[which], diag_ref, sems.at[4]),
+    ]
+    for copy in blocks:
+        copy.start()
+    coup.wait()
+    for copy in blocks:
+        copy.wait()
+    zero = jnp.zeros((), jnp.bfloat16)
+    full = jnp.where(keep(count, 0, BLK), gen_ref[...], zero)
+    col_ref[0] = lax.dot_general(
+        coup_ref[...], full, (((0,), (1,)), ((), ())), preferred_element_type=jnp.float32
+    ).astype(jnp.bfloat16)
+    lanes = lax.broadcasted_iota(jnp.int32, (BLK, BLK), 1) < count
+    col_ref[1] = jnp.where(keep(count, 0, BLK) & lanes, diag_ref[...], zero)
+
+
+def fetch_kernel(par_ref, out_ref):
+    a = pl.program_id(0)
+    for b in range(4):
+        for half in range(2):
+            out_ref[a, b, :, 128 * half : 128 * half + 128] = par_ref[0, pl.ds(4 * half + b, BLK, stride=8), :]
 
 
 def join_kernel(
@@ -139,10 +180,10 @@
 
     left = rows_ref[a]
     for b in range(4):
-        tile = jnp.dot(left, cols_ref[b], preferred_element_type=jnp.float32)
+        tile = par_ref[a, b] + jnp.dot(left, cols_ref[b], preferred_element_type=jnp.float32)
         for half in range(2):
             at = pl.ds(4 * half + b, BLK, stride=8)
-            out_ref[0, at, :] = par_ref[0, at, :] + tile[:, 128 * half : 128 * half + 128]
+            out_ref[0, at, :] = tile[:, 128 * half : 128 * half + 128]
 
     t = z * X + x
     row = 2 * y + k
@@ -159,57 +200,84 @@
                     out_ref[0, at, :] = out_ref[0, at, :] + both[:, 128 * half : 128 * half + 128]
 
 
-def shards(parent_front, generators, diagonal_blocks, coupling, block_map, valid_rows):
+def limits(mib, flops=0, moved=0):
+    return dict(
+        compiler_params=pltpu.CompilerParams(vmem_limit_bytes=mib * 2**20),
+        cost_estimate=pl.CostEstimate(flops=flops, bytes_accessed=moved, transcendentals=0),
+    )
+
+
+def assemble(parent_front, generators, diagonal_blocks, coupling, block_map, valid_rows):
     bf16 = jnp.bfloat16
     vmem = pl.BlockSpec(memory_space=pltpu.VMEM)
-    smem = pl.BlockSpec(memory_space=pltpu.SMEM)
-    loc, rem, send, col = pl.pallas_call(
-        pack_kernel,
+    hbm = pl.BlockSpec(memory_space=pltpu.HBM)
+    block_map, valid_rows, generators, diagonal_blocks, coupling = (
+        pltpu.with_memory_space_constraint(v, pltpu.HBM)
+        for v in (block_map, valid_rows, generators, diagonal_blocks, coupling)
+    )
+    tables = [pltpu.SMEM(block_map.shape, jnp.int32)] * 2
+    loc, rem, send = pl.pallas_call(
+        rows_kernel,
         out_shape=(
             jax.ShapeDtypeStruct((2, BLK, BLK), bf16),
             jax.ShapeDtypeStruct((3, 2, 2, QUART, BLK), bf16),
             jax.ShapeDtypeStruct((14, 2 * QUART, BLK), bf16),
-            jax.ShapeDtypeStruct((2, BLK, BLK), bf16),
         ),
-        in_specs=[smem, smem, vmem, vmem, vmem],
-        out_specs=(vmem, vmem, vmem, vmem),
-        compiler_params=pltpu.CompilerParams(vmem_limit_bytes=16 * 2**20),
+        in_specs=[hbm] * 3,
+        out_specs=(vmem,) * 3,
+        scratch_shapes=tables + [pltpu.VMEM(generators.shape, bf16), pltpu.SemaphoreType.DMA((3,))],
+        **limits(8, 10**6, 2**21),
+    )(block_map, valid_rows, generators)
+    col = pl.pallas_call(
+        column_kernel,
+        out_shape=jax.ShapeDtypeStruct((2, BLK, BLK), bf16),
+        in_specs=[hbm] * 5,
+        out_specs=vmem,
+        scratch_shapes=tables + [pltpu.VMEM((BLK, BLK), bf16)] * 3 + [pltpu.SemaphoreType.DMA((5,))],
+        **limits(4, 2 * BLK**3, 2**19),
     )(block_map, valid_rows, generators, diagonal_blocks, coupling)
 
     flip = lambda y, k, z, x: (y, 1 - k, z, x)
     swap = shift(send, flip)
-    got = []
+    got = {}
     for step in (1, 3, 2):
         there = swap[2 * step - 2 : 2 * step].reshape(2, 2, QUART, BLK).swapaxes(0, 1)
         payload = jnp.concatenate([rem[step - 1], there], axis=1)
-        got.append(shift(payload, lambda y, k, z, x, n=step: (y + n, k, z, x)))
-    got = [got[0], got[2], got[1]]
-    cols = [col] + [shift(col, lambda y, k, z, x, n=step: (y + n, k, z, x)) for step in (1, 2, 3)]
+        got[step] = shift(payload, lambda y, k, z, x, n=step: (y + n, k, z, x))
+    cols = [col] + [shift(col, lambda y, k, z, x, n=n: (y + n, k, z, x)) for n in (1, 2, 3)]
     others = [shift(c, flip) for c in cols]
-    for_x = jnp.stack([g[0] for g in got])
-    for_z = jnp.stack([g[1] for g in got])
-    xs = [shift(for_x, lambda y, k, z, x, n=far: (y, k, z, x + n)) for far in (1, 2, 3)]
-    zs = [shift(for_z, lambda y, k, z, x, n=far: (y, k, z + n, x)) for far in (1, 2, 3)]
+    for_x = jnp.stack([got[n][0] for n in (1, 2, 3)])
+    for_z = jnp.stack([got[n][1] for n in (1, 2, 3)])
+    xs = [shift(for_x, lambda y, k, z, x, n=n: (y, k, z, x + n)) for n in (1, 2, 3)]
+    zs = [shift(for_z, lambda y, k, z, x, n=n: (y, k, z + n, x)) for n in (1, 2, 3)]
 
     a_count = parent_front.shape[0]
     flat = parent_front.reshape(a_count, BLK, 4, 2, 128).transpose(0, 1, 3, 2, 4).reshape(a_count, BLK * 8, 128)
     block = pl.BlockSpec((1, BLK * 8, 128), lambda a: (a, 0, 0))
+    front = pl.pallas_call(
+        fetch_kernel,
+        grid=(a_count,),
+        out_shape=jax.ShapeDtypeStruct((a_count, 4, BLK, BLK), jnp.float32),
+        in_specs=[block],
+        out_specs=vmem,
+        **limits(16, 10**9, 2**23),
+    )(flat)
     joined = pl.pallas_call(
         join_kernel,
         grid=(a_count,),
         out_shape=jax.ShapeDtypeStruct(flat.shape, jnp.float32),
-        in_specs=[block] + [vmem] * 19,
+        in_specs=[vmem] * 20,
         out_specs=block,
         scratch_shapes=[
             pltpu.VMEM((a_count, BLK, 2 * BLK), bf16),
             pltpu.VMEM((4, 2 * BLK, BLK), bf16),
         ],
-        compiler_params=pltpu.CompilerParams(vmem_limit_bytes=32 * 2**20),
-    )(flat, loc, swap, *got, *xs, *zs, *cols, *others)
+        **limits(24, 2**31, 2**24),
+    )(front, loc, swap, got[1], got[2], got[3], *xs, *zs, *cols, *others)
     return joined.reshape(a_count, BLK, 2, 4, 128).transpose(0, 1, 3, 2, 4).reshape(parent_front.shape)
 
 
 def solution(mesh):
     in_specs = (P(None, "row", None, "col"), P("row", None, None), P("row", None, None), P(), P(), P())
     out_specs = P(None, "row", None, "col")
-    return jax.shard_map(shards, mesh=mesh, in_specs=in_specs, out_specs=out_specs, check_vma=False)
+    return jax.shard_map(assemble, mesh=mesh, in_specs=in_specs, out_specs=out_specs, check_vma=False)

time: 73.2 us -> 67.1 us (0.917)
  local copies, waits for them, and re-layouts: 8.58 us -> 0.08 us
  Pallas kernels: 8.88 us -> 13 us
  waiting for transfers between devices: 39.2 us -> 37.6 us
    unnamed x12 -> x2, local copies, waits for them, and re-layouts: 8.5 us -> 0.01 us
    pallas_call x2 -> x4, Pallas kernels: 8.88 us -> 13 us  [the longest x1 6.96 us: assemble(): pl.pallas_call(join_kernel, grid=(a_count,), out_shape=jax.ShapeDtypeStru...]
    ppermute x17, waiting for transfers between devices: 39.2 us -> 37.6 us  [shift(): return lax.ppermute(value, ('row', 'col'), pairs(move))]
  transfers between devices with their start and end apart: 17 -> 17, of which waited for: 10 -> 10; matrix products, arithmetic and copies ran while one was open for 0% -> 0% of each run, Pallas kernels for 0% -> 6%
where the time goes in v2:
time: 67.1 us; the launch traced here: 66.9 us
  waiting for transfers between devices  37.6 us (56%)
  starting transfers between devices  16 us (24%)
  Pallas kernels  13 us (19%)
    ppermute x17, waiting for transfers between devices, shift(): return lax.ppermute(value, ('row', 'col'), pairs(move))  37.6 us
    ppermute x17, starting transfers between devices, shift(): return lax.ppermute(value, ('row', 'col'), pairs(move))  16 us
    pallas_call x1, Pallas kernels, assemble(): pl.pallas_call(join_kernel, grid=(a_count,), out_shape=jax.ShapeDtypeStru...  6.96 us
    pallas_call x1, Pallas kernels, assemble(): pl.pallas_call(rows_kernel, out_shape=(jax.ShapeDtypeStruct((2, BLK, BLK)...  2.2 us
    pallas_call x1, Pallas kernels, assemble(): pl.pallas_call(column_kernel, out_shape=jax.ShapeDtypeStruct((2, BLK, BLK...  2.15 us
    pallas_call x1, Pallas kernels, assemble(): pl.pallas_call(fetch_kernel, grid=(a_count,), out_shape=jax.ShapeDtypeStr...  1.66 us
  transfers between devices with their start and end apart: 17, of which 10 were waited for; matrix products, arithmetic and copies ran while one was open for 0% of the time, Pallas kernels for 6%

profile of v2, /device:TPU:0, one launch (start us, length us, event | category | flops | bytes accessed | tf_op | source)
XLA Modules:
  0.0 66.9 jit_solution(17693508063540352712)
XLA Ops:
  0.0 0.0 copy-start
  0.0 2.2 %shard_map.65 = (bf16[2,256,256]{2,1,0:T(8,128)(2,1)S(1)}, bf16[3,2,2,32,256]{4,3,2,1,0:T(8,128)(2,1)S(1)}, bf16[14,64,256]{2,1,0:T(8,128)(2,1)S(1)}) custom-call(s32[2,48]{1,0:T(2,128)} %map_hbm.3, s32[2,48]{1,0:T(2,128)} %count_hbm.3, bf16[12,256,256]{2,1,0:T(8,128)(2,1)} %gen_hbm.3), custom_call_target="tpu_custom_call" | custom-call | flops 1000000 | bytes 2097152 | tf_op jit(solution)/shard_map/pallas_call | solution.py:219
  2.2 0.1 collective-permute-start
  2.3 2.2 %shard_map.66.c0 = bf16[2,256,256]{2,1,0:T(8,128)(2,1)S(1)} custom-call(s32[2,48]{1,0:T(2,128)} %map_hbm.3, s32[2,48]{1,0:T(2,128)} %count_hbm.3, bf16[12,256,256]{2,1,0:T(8,128)(2,1)} %gen_hbm.3, bf16[12,256,256]{2,1,0:T(8,128)(2,1)} %diag_hbm.1, bf16[2,256,256]{2,1,0:T(8,128)(2,1)} %coup_hbm.1), custom_call_target="tpu_custom_call" | custom-call | flops 33554432 | bytes 524288 | tf_op jit(solution)/shard_map/pallas_call | solution.py:231
  4.5 3.2 %collective-permute-start.12 = (bf16[2,256,256]{2,1,0:T(8,128)(2,1)S(1)}, bf16[2,256,256]{2,1,0:T(8,128)(2,1)S(1)}, u32[]{:S(2)}, u32[]{:S(2)}) collective-permute-start(bf16[2,256,256]{2,1,0:T(8,128)(2,1)S(1)} %shard_map.66.c0), channel_id=1, source_target_pairs={{0,96},{1,97},{2,98},{3,99},{4,100},{5,101},{6,102},{7,103},{8,104... | collective-permute-start | bytes 786440 | tf_op jit(solution)/shard_map/ppermute | solution.py:28
  7.6 0.6 collective-permute-start.11
  8.3 1.0 %collective-permute-start.10 = (bf16[2,256,256]{2,1,0:T(8,128)(2,1)S(1)}, bf16[2,256,256]{2,1,0:T(8,128)(2,1)S(1)}, u32[]{:S(2)}, u32[]{:S(2)}) collective-permute-start(bf16[2,256,256]{2,1,0:T(8,128)(2,1)S(1)} %shard_map.66.c0), channel_id=1, source_target_pairs={{0,32},{1,33},{2,34},{3,35},{4,36},{5,37},{6,38},{7,39},{8,40},{9,... | collective-permute-start | bytes 786440 | tf_op jit(solution)/shard_map/ppermute | solution.py:28
  9.2 0.0 collective-permute-start.13
  9.3 10.2 %collective-permute-done.12.c3 = bf16[2,256,256]{2,1,0:T(8,128)(2,1)S(1)} collective-permute-done((bf16[2,256,256]{2,1,0:T(8,128)(2,1)S(1)}, bf16[2,256,256]{2,1,0:T(8,128)(2,1)S(1)}, u32[]{:S(2)}, u32[]{:S(2)}) %collective-permute-start.12) | collective-permute-done | bytes 262176 | tf_op jit(solution)/shard_map/ppermute | solution.py:28
  19.4 0.0 collective-permute-start.16
  19.4 0.0 collective-permute-done.11.c2
  19.4 0.5 collective-permute-start.15
  20.0 3.2 %collective-permute-done.10.c1 = bf16[2,256,256]{2,1,0:T(8,128)(2,1)S(1)} collective-permute-done((bf16[2,256,256]{2,1,0:T(8,128)(2,1)S(1)}, bf16[2,256,256]{2,1,0:T(8,128)(2,1)S(1)}, u32[]{:S(2)}, u32[]{:S(2)}) %collective-permute-start.10) | collective-permute-done | bytes 262176 | tf_op jit(solution)/shard_map/ppermute | solution.py:28
  23.1 0.0 collective-permute-start.14
  23.2 0.0 collective-permute-done.swap_ref
  23.2 0.1 collective-permute-start.1
  23.4 7.0 %collective-permute-done.1.r1 = bf16[2,4,32,256]{3,2,1,0:T(8,128)(2,1)S(1)} collective-permute-done((bf16[2,4,32,256]{3,2,1,0:T(8,128)(2,1)S(1)}, bf16[2,4,32,256]{3,2,1,0:T(8,128)(2,1)S(1)}, u32[]{:S(2)}, u32[]{:S(2)}) %collective-permute-start.1) | collective-permute-done | bytes 131104 | tf_op jit(solution)/shard_map/ppermute | solution.py:28
  30.4 0.0 collective-permute-start.2
  30.4 6.5 %collective-permute-done.2.r2 = bf16[2,4,32,256]{3,2,1,0:T(8,128)(2,1)S(1)} collective-permute-done((bf16[2,4,32,256]{3,2,1,0:T(8,128)(2,1)S(1)}, bf16[2,4,32,256]{3,2,1,0:T(8,128)(2,1)S(1)}, u32[]{:S(2)}, u32[]{:S(2)}) %collective-permute-start.2) | collective-permute-done | bytes 131104 | tf_op jit(solution)/shard_map/ppermute | solution.py:28
  37.0 0.0 collective-permute-start.3
  37.0 5.0 %collective-permute-done.3.r3 = bf16[2,4,32,256]{3,2,1,0:T(8,128)(2,1)S(1)} collective-permute-done((bf16[2,4,32,256]{3,2,1,0:T(8,128)(2,1)S(1)}, bf16[2,4,32,256]{3,2,1,0:T(8,128)(2,1)S(1)}, u32[]{:S(2)}, u32[]{:S(2)}) %collective-permute-start.3) | collective-permute-done | bytes 131104 | tf_op jit(solution)/shard_map/ppermute | solution.py:28
  42.0 2.8 %collective-permute-start.6 = (bf16[3,4,32,256]{3,2,1,0:T(8,128)(2,1)S(1)}, bf16[3,4,32,256]{3,2,1,0:T(8,128)(2,1)S(1)}, u32[]{:S(2)}, u32[]{:S(2)}) collective-permute-start(bf16[3,4,32,256]{3,2,1,0:T(8,128)(2,1)S(1)} %pad_maximum_fusion), channel_id=1, source_target_pairs={{0,3},{1,0},{2,1},{3,2},{4,7},{5,4},{6,5},{7,6},{8,11},{9,8},{10,9... | collective-permute-start | bytes 589832 | tf_op jit(solution)/shard_map/ppermute | solution.py:28
  44.8 0.0 collective-permute-done.13.d0
  44.8 0.9 %collective-permute-start.5 = (bf16[3,4,32,256]{3,2,1,0:T(8,128)(2,1)S(1)}, bf16[3,4,32,256]{3,2,1,0:T(8,128)(2,1)S(1)}, u32[]{:S(2)}, u32[]{:S(2)}) collective-permute-start(bf16[3,4,32,256]{3,2,1,0:T(8,128)(2,1)S(1)} %pad_maximum_fusion), channel_id=1, source_target_pairs={{0,2},{1,3},{2,0},{3,1},{4,6},{5,7},{6,4},{7,5},{8,10},{9,11},{10,... | collective-permute-start | bytes 589832 | tf_op jit(solution)/shard_map/ppermute | solution.py:28
  45.7 0.0 collective-permute-done.16.d3
  45.7 0.9 %collective-permute-start.4 = (bf16[3,4,32,256]{3,2,1,0:T(8,128)(2,1)S(1)}, bf16[3,4,32,256]{3,2,1,0:T(8,128)(2,1)S(1)}, u32[]{:S(2)}, u32[]{:S(2)}) collective-permute-start(bf16[3,4,32,256]{3,2,1,0:T(8,128)(2,1)S(1)} %pad_maximum_fusion), channel_id=1, source_target_pairs={{0,1},{1,2},{2,3},{3,0},{4,5},{5,6},{6,7},{7,4},{8,9},{9,10},{10,1... | collective-permute-start | bytes 589832 | tf_op jit(solution)/shard_map/ppermute | solution.py:28
  46.6 0.0 collective-permute-done.15.d2
  46.6 4.0 %collective-permute-start.9 = (bf16[3,4,32,256]{3,2,1,0:T(8,128)(2,1)S(1)}, bf16[3,4,32,256]{3,2,1,0:T(8,128)(2,1)S(1)}, u32[]{:S(2)}, u32[]{:S(2)}) collective-permute-start(bf16[3,4,32,256]{3,2,1,0:T(8,128)(2,1)S(1)} %pad_maximum_fusion.1), channel_id=1, source_target_pairs={{0,12},{1,13},{2,14},{3,15},{4,0},{5,1},{6,2},{7,3},{8,4},{9,5},{1... | collective-permute-start | bytes 589832 | tf_op jit(solution)/shard_map/ppermute | solution.py:28
  50.6 0.0 collective-permute-done.14.d1
  50.6 0.0 collective-permute-start.8
  50.7 0.4 collective-permute-done.6.x3
  51.0 1.9 %collective-permute-start.7 = (bf16[3,4,32,256]{3,2,1,0:T(8,128)(2,1)S(1)}, bf16[3,4,32,256]{3,2,1,0:T(8,128)(2,1)S(1)}, u32[]{:S(2)}, u32[]{:S(2)}) collective-permute-start(bf16[3,4,32,256]{3,2,1,0:T(8,128)(2,1)S(1)} %pad_maximum_fusion.1), channel_id=1, source_target_pairs={{0,4},{1,5},{2,6},{3,7},{4,8},{5,9},{6,10},{7,11},{8,12},{9,13},{1... | collective-permute-start | bytes 589832 | tf_op jit(solution)/shard_map/ppermute | solution.py:28
  52.9 0.0 copy-done
  52.9 1.7 %shard_map.64.par_ref = f32[8,4,256,256]{3,2,1,0:T(8,128)S(1)} custom-call(f32[8,2048,128]{2,1,0:T(8,128)S(1)} %bitcast.28), custom_call_target="tpu_custom_call" | custom-call | flops 1000000000 | bytes 8388608 | tf_op jit(solution)/shard_map/pallas_call | solution.py:257
  54.6 0.0 collective-permute-done.5.x2
  54.6 0.2 collective-permute-done.4.x1
  54.8 1.2 %collective-permute-done.9.z3 = bf16[3,4,32,256]{3,2,1,0:T(8,128)(2,1)S(1)} collective-permute-done((bf16[3,4,32,256]{3,2,1,0:T(8,128)(2,1)S(1)}, bf16[3,4,32,256]{3,2,1,0:T(8,128)(2,1)S(1)}, u32[]{:S(2)}, u32[]{:S(2)}) %collective-permute-start.9) | collective-permute-done | bytes 196640 | tf_op jit(solution)/shard_map/ppermute | solution.py:28
  56.0 1.9 %collective-permute-done.8.z2 = bf16[3,4,32,256]{3,2,1,0:T(8,128)(2,1)S(1)} collective-permute-done((bf16[3,4,32,256]{3,2,1,0:T(8,128)(2,1)S(1)}, bf16[3,4,32,256]{3,2,1,0:T(8,128)(2,1)S(1)}, u32[]{:S(2)}, u32[]{:S(2)}) %collective-permute-start.8) | collective-permute-done | bytes 196640 | tf_op jit(solution)/shard_map/ppermute | solution.py:28
  57.9 2.0 %collective-permute-done.7.z1 = bf16[3,4,32,256]{3,2,1,0:T(8,128)(2,1)S(1)} collective-permute-done((bf16[3,4,32,256]{3,2,1,0:T(8,128)(2,1)S(1)}, bf16[3,4,32,256]{3,2,1,0:T(8,128)(2,1)S(1)}, u32[]{:S(2)}, u32[]{:S(2)}) %collective-permute-start.7) | collective-permute-done | bytes 196640 | tf_op jit(solution)/shard_map/ppermute | solution.py:28
  59.9 7.0 %shard_map.67 = f32[8,2048,128]{2,1,0:T(8,128)} custom-call(f32[8,4,256,256]{3,2,1,0:T(8,128)S(1)} %shard_map.64.par_ref, bf16[2,256,256]{2,1,0:T(8,128)(2,1)S(1)} %get-tuple-element.8.loc_ref, bf16[14,64,256]{2,1,0:T(8,128)(2,1)S(1)} %collective-permute-done.swap_ref, bf16[2,4,32,256]{3,2,1,0:T(8,128)(2,1)S(1)} %collective-permute-done.1.r1, ...), custom_call_target="tpu_custom_call" | custom-call | flops 2147483648 | bytes 16777216 | tf_op jit(solution)/shard_map/pallas_call | solution.py:265
  (13 shorter events, 0.2 us)
Async XLA Ops:
  0.0 52.9 %copy-start = (f32[8,256,4,256]{3,2,1,0:T(4,128)S(1)}, f32[8,256,4,256]{3,2,1,0:T(4,128)}, u32[]{:S(2)}) copy-start(f32[8,256,4,256]{3,2,1,0:T(4,128)} %param.6) | copy-start | bytes 25165828
  2.2 21.0 %collective-permute-start = (bf16[14,64,256]{2,1,0:T(8,128)(2,1)S(1)}, bf16[14,64,256]{2,1,0:T(8,128)(2,1)S(1)}, u32[]{:S(2)}, u32[]{:S(2)}) collective-permute-start(bf16[14,64,256]{2,1,0:T(8,128)(2,1)S(1)} %get-tuple-element.9), channel_id=1, source_target_pairs={{0,16},{1,17},{2,18},{3,19},{4,20},{5,21},{6,22},{7,23},{8,24},{9,... | collective-permute-start | bytes 1376264 | tf_op jit(solution)/shard_map/ppermute | solution.py:28
  4.5 15.0 %collective-permute-start.12 = (bf16[2,256,256]{2,1,0:T(8,128)(2,1)S(1)}, bf16[2,256,256]{2,1,0:T(8,128)(2,1)S(1)}, u32[]{:S(2)}, u32[]{:S(2)}) collective-permute-start(bf16[2,256,256]{2,1,0:T(8,128)(2,1)S(1)} %shard_map.66.c0), channel_id=1, source_target_pairs={{0,96},{1,97},{2,98},{3,99},{4,100},{5,101},{6,102},{7,103},{8,104... | collective-permute-start | bytes 786440 | tf_op jit(solution)/shard_map/ppermute | solution.py:28
  7.6 11.8 %collective-permute-start.11 = (bf16[2,256,256]{2,1,0:T(8,128)(2,1)S(1)}, bf16[2,256,256]{2,1,0:T(8,128)(2,1)S(1)}, u32[]{:S(2)}, u32[]{:S(2)}) collective-permute-start(bf16[2,256,256]{2,1,0:T(8,128)(2,1)S(1)} %shard_map.66.c0), channel_id=1, source_target_pairs={{0,64},{1,65},{2,66},{3,67},{4,68},{5,69},{6,70},{7,71},{8,72},{9,... | collective-permute-start | bytes 786440 | tf_op jit(solution)/shard_map/ppermute | solution.py:28
  8.3 14.9 %collective-permute-start.10 = (bf16[2,256,256]{2,1,0:T(8,128)(2,1)S(1)}, bf16[2,256,256]{2,1,0:T(8,128)(2,1)S(1)}, u32[]{:S(2)}, u32[]{:S(2)}) collective-permute-start(bf16[2,256,256]{2,1,0:T(8,128)(2,1)S(1)} %shard_map.66.c0), channel_id=1, source_target_pairs={{0,32},{1,33},{2,34},{3,35},{4,36},{5,37},{6,38},{7,39},{8,40},{9,... | collective-permute-start | bytes 786440 | tf_op jit(solution)/shard_map/ppermute | solution.py:28
  9.2 35.6 %collective-permute-start.13 = (bf16[2,256,256]{2,1,0:T(8,128)(2,1)S(1)}, bf16[2,256,256]{2,1,0:T(8,128)(2,1)S(1)}, u32[]{:S(2)}, u32[]{:S(2)}) collective-permute-start(bf16[2,256,256]{2,1,0:T(8,128)(2,1)S(1)} %shard_map.66.c0), channel_id=1, source_target_pairs={{0,16},{1,17},{2,18},{3,19},{4,20},{5,21},{6,22},{7,23},{8,24},{9,... | collective-permute-start | bytes 786440 | tf_op jit(solution)/shard_map/ppermute | solution.py:28
  19.4 26.3 %collective-permute-start.16 = (bf16[2,256,256]{2,1,0:T(8,128)(2,1)S(1)}, bf16[2,256,256]{2,1,0:T(8,128)(2,1)S(1)}, u32[]{:S(2)}, u32[]{:S(2)}) collective-permute-start(bf16[2,256,256]{2,1,0:T(8,128)(2,1)S(1)} %collective-permute-done.12.c3), channel_id=1, source_target_pairs={{0,16},{1,17},{2,18},{3,19},{4,20},{5,21},{6,22},{7,23},{8,24},{9,... | collective-permute-start | bytes 786440 | tf_op jit(solution)/shard_map/ppermute | solution.py:28
  19.4 27.2 %collective-permute-start.15 = (bf16[2,256,256]{2,1,0:T(8,128)(2,1)S(1)}, bf16[2,256,256]{2,1,0:T(8,128)(2,1)S(1)}, u32[]{:S(2)}, u32[]{:S(2)}) collective-permute-start(bf16[2,256,256]{2,1,0:T(8,128)(2,1)S(1)} %collective-permute-done.11.c2), channel_id=1, source_target_pairs={{0,16},{1,17},{2,18},{3,19},{4,20},{5,21},{6,22},{7,23},{8,24},{9,... | collective-permute-start | bytes 786440 | tf_op jit(solution)/shard_map/ppermute | solution.py:28
  23.1 27.5 %collective-permute-start.14 = (bf16[2,256,256]{2,1,0:T(8,128)(2,1)S(1)}, bf16[2,256,256]{2,1,0:T(8,128)(2,1)S(1)}, u32[]{:S(2)}, u32[]{:S(2)}) collective-permute-start(bf16[2,256,256]{2,1,0:T(8,128)(2,1)S(1)} %collective-permute-done.10.c1), channel_id=1, source_target_pairs={{0,16},{1,17},{2,18},{3,19},{4,20},{5,21},{6,22},{7,23},{8,24},{9,... | collective-permute-start | bytes 786440 | tf_op jit(solution)/shard_map/ppermute | solution.py:28
  23.2 7.2 %collective-permute-start.1 = (bf16[2,4,32,256]{3,2,1,0:T(8,128)(2,1)S(1)}, bf16[2,4,32,256]{3,2,1,0:T(8,128)(2,1)S(1)}, u32[]{:S(2)}, u32[]{:S(2)}) collective-permute-start(bf16[2,4,32,256]{3,2,1,0:T(8,128)(2,1)S(1)} %pad_maximum_fusion.2), channel_id=1, source_target_pairs={{0,32},{1,33},{2,34},{3,35},{4,36},{5,37},{6,38},{7,39},{8,40},{9,... | collective-permute-start | bytes 393224 | tf_op jit(solution)/shard_map/ppermute | solution.py:28
  30.4 6.5 %collective-permute-start.2 = (bf16[2,4,32,256]{3,2,1,0:T(8,128)(2,1)S(1)}, bf16[2,4,32,256]{3,2,1,0:T(8,128)(2,1)S(1)}, u32[]{:S(2)}, u32[]{:S(2)}) collective-permute-start(bf16[2,4,32,256]{3,2,1,0:T(8,128)(2,1)S(1)} %pad_maximum_fusion.3), channel_id=1, source_target_pairs={{0,64},{1,65},{2,66},{3,67},{4,68},{5,69},{6,70},{7,71},{8,72},{9,... | collective-permute-start | bytes 393224 | tf_op jit(solution)/shard_map/ppermute | solution.py:28
  37.0 5.0 %collective-permute-start.3 = (bf16[2,4,32,256]{3,2,1,0:T(8,128)(2,1)S(1)}, bf16[2,4,32,256]{3,2,1,0:T(8,128)(2,1)S(1)}, u32[]{:S(2)}, u32[]{:S(2)}) collective-permute-start(bf16[2,4,32,256]{3,2,1,0:T(8,128)(2,1)S(1)} %pad_maximum_fusion.4), channel_id=1, source_target_pairs={{0,96},{1,97},{2,98},{3,99},{4,100},{5,101},{6,102},{7,103},{8,104... | collective-permute-start | bytes 393224 | tf_op jit(solution)/shard_map/ppermute | solution.py:28
  42.0 9.0 %collective-permute-start.6 = (bf16[3,4,32,256]{3,2,1,0:T(8,128)(2,1)S(1)}, bf16[3,4,32,256]{3,2,1,0:T(8,128)(2,1)S(1)}, u32[]{:S(2)}, u32[]{:S(2)}) collective-permute-start(bf16[3,4,32,256]{3,2,1,0:T(8,128)(2,1)S(1)} %pad_maximum_fusion), channel_id=1, source_target_pairs={{0,3},{1,0},{2,1},{3,2},{4,7},{5,4},{6,5},{7,6},{8,11},{9,8},{10,9... | collective-permute-start | bytes 589832 | tf_op jit(solution)/shard_map/ppermute | solution.py:28
  44.8 9.8 %collective-permute-start.5 = (bf16[3,4,32,256]{3,2,1,0:T(8,128)(2,1)S(1)}, bf16[3,4,32,256]{3,2,1,0:T(8,128)(2,1)S(1)}, u32[]{:S(2)}, u32[]{:S(2)}) collective-permute-start(bf16[3,4,32,256]{3,2,1,0:T(8,128)(2,1)S(1)} %pad_maximum_fusion), channel_id=1, source_target_pairs={{0,2},{1,3},{2,0},{3,1},{4,6},{5,7},{6,4},{7,5},{8,10},{9,11},{10,... | collective-permute-start | bytes 589832 | tf_op jit(solution)/shard_map/ppermute | solution.py:28
  45.7 9.1 %collective-permute-start.4 = (bf16[3,4,32,256]{3,2,1,0:T(8,128)(2,1)S(1)}, bf16[3,4,32,256]{3,2,1,0:T(8,128)(2,1)S(1)}, u32[]{:S(2)}, u32[]{:S(2)}) collective-permute-start(bf16[3,4,32,256]{3,2,1,0:T(8,128)(2,1)S(1)} %pad_maximum_fusion), channel_id=1, source_target_pairs={{0,1},{1,2},{2,3},{3,0},{4,5},{5,6},{6,7},{7,4},{8,9},{9,10},{10,1... | collective-permute-start | bytes 589832 | tf_op jit(solution)/shard_map/ppermute | solution.py:28
  46.6 9.4 %collective-permute-start.9 = (bf16[3,4,32,256]{3,2,1,0:T(8,128)(2,1)S(1)}, bf16[3,4,32,256]{3,2,1,0:T(8,128)(2,1)S(1)}, u32[]{:S(2)}, u32[]{:S(2)}) collective-permute-start(bf16[3,4,32,256]{3,2,1,0:T(8,128)(2,1)S(1)} %pad_maximum_fusion.1), channel_id=1, source_target_pairs={{0,12},{1,13},{2,14},{3,15},{4,0},{5,1},{6,2},{7,3},{8,4},{9,5},{1... | collective-permute-start | bytes 589832 | tf_op jit(solution)/shard_map/ppermute | solution.py:28
  50.6 7.3 %collective-permute-start.8 = (bf16[3,4,32,256]{3,2,1,0:T(8,128)(2,1)S(1)}, bf16[3,4,32,256]{3,2,1,0:T(8,128)(2,1)S(1)}, u32[]{:S(2)}, u32[]{:S(2)}) collective-permute-start(bf16[3,4,32,256]{3,2,1,0:T(8,128)(2,1)S(1)} %pad_maximum_fusion.1), channel_id=1, source_target_pairs={{0,8},{1,9},{2,10},{3,11},{4,12},{5,13},{6,14},{7,15},{8,0},{9,1},... | collective-permute-start | bytes 589832 | tf_op jit(solution)/shard_map/ppermute | solution.py:28
  51.0 8.9 %collective-permute-start.7 = (bf16[3,4,32,256]{3,2,1,0:T(8,128)(2,1)S(1)}, bf16[3,4,32,256]{3,2,1,0:T(8,128)(2,1)S(1)}, u32[]{:S(2)}, u32[]{:S(2)}) collective-permute-start(bf16[3,4,32,256]{3,2,1,0:T(8,128)(2,1)S(1)} %pad_maximum_fusion.1), channel_id=1, source_target_pairs={{0,4},{1,5},{2,6},{3,7},{4,8},{5,9},{6,10},{7,11},{8,12},{9,13},{1... | collective-permute-start | bytes 589832 | tf_op jit(solution)/shard_map/ppermute | solution.py:28
